TPU v7x, 256 devices: a whole 4x4x8 slice. The times are simulated.
256 devices in a mesh: gx: 8 (over z), gy: 8 (over y_lo, x), gz: 4 (over y_hi, core).
Axes of the slice: x: 4, y: 4 (y_hi: 2, y_lo: 2; y = y_hi * 2 + y_lo), z: 8, core: 2. Of those that a mesh axis runs over, the one named last changes fastest.
Arguments:
- constraint: bfloat16 [8, 8, 4, 256, 3072], P('gx', 'gy', 'gz'), may hold values from -1.5 to 1.5
- stiff_ib: bfloat16 [8, 8, 4, 256, 3072], P('gx', 'gy', 'gz'), may hold values from -0.75 to 0.75
- mass_ib: bfloat16 [8, 8, 4, 256, 3072], P('gx', 'gy', 'gz'), may hold values from -1.5 to 1.5
- mass_ii: float32 [8, 8, 4, 256], P('gx', 'gy', 'gz'), may hold values from 0.5 to 4
- modes: bfloat16 [8, 8, 4, 300, 256], P('gx', 'gy', 'gz'), may hold values from -0.375 to 0.375
- stiff_faces: bfloat16 [8, 8, 4, 6, 512, 512], P('gx', 'gy', 'gz'), may hold values from -3 to 3
- mass_faces: bfloat16 [8, 8, 4, 6, 512], P('gx', 'gy', 'gz'), may hold values from 0.19921875 to 4
- dof_map: int32 [8, 8, 4, 3, 512], P('gx', 'gy', 'gz'), may hold values from 0 to 511, each once within a row
Outputs:
- stiff_assembled: bfloat16 [8, 8, 4, 3, 512, 512], P('gx', 'gy', 'gz')
- mass_assembled: bfloat16 [8, 8, 4, 3, 512, 512], P('gx', 'gy', 'gz')
- modal_coupling: bfloat16 [8, 8, 4, 3, 600, 512], P('gx', 'gy', 'gz')
Inputs may be any that keep to these rules, and one draw needn't show every extreme that they name: `dof_map`: each row of the last dimension is a permutation of 0 to 511.
All inputs are finite; a program needn't handle non-finite values.
Results may differ from a plain program's by a relative error of at most 0.0075.
Values may be sent and summed in bfloat16 or wider, within the bound.
A program may use at most 64 MiB of HBM per device.

v0:
```python
import jax
import jax.numpy as jnp
from jax import lax
from jax.sharding import PartitionSpec as P


def shifted(block, axis, distance):
    devices = range(lax.axis_size(axis))
    route = [(i - distance, i) for i in devices if i - distance in devices]
    return lax.ppermute(block, axis, route)


def transposed(left, right):
    return lax.dot_general(
        left, right, (((0,), (0,)), ((), ())), preferred_element_type=jnp.float32
    )


def by_rows_t(left, right):
    return lax.dot_general(
        left, right, (((1,), (1,)), ((), ())), preferred_element_type=jnp.float32
    )


def reduce_face(stiff_cols, mass_cols, cons_cols, load_cols, modes, stiff_face, mass_face):
    stiff_block = (stiff_face.astype(jnp.float32) + transposed(stiff_cols, cons_cols)).astype(
        jnp.bfloat16
    )
    mass_block = (
        jnp.diag(mass_face.astype(jnp.float32))
        + transposed(cons_cols, load_cols)
        + transposed(mass_cols, cons_cols)
    ).astype(jnp.bfloat16)
    coup_block = jnp.dot(modes, load_cols, preferred_element_type=jnp.float32).astype(jnp.bfloat16)
    return (stiff_block, mass_block, coup_block)


def face_columns(face, stiff_ib, mass_ib, constraint, loaded, modes, stiff_faces, mass_faces):
    width = stiff_faces.shape[-1]
    lower = face * width
    return (
        stiff_ib[:, lower : lower + width],
        mass_ib[:, lower : lower + width],
        constraint[:, lower : lower + width],
        loaded[:, lower : lower + width],
        modes,
        stiff_faces[face],
        mass_faces[face],
    )


def reorder_both(matrix, select):
    rows_first = jnp.dot(select, matrix, preferred_element_type=jnp.float32).astype(jnp.bfloat16)
    return by_rows_t(rows_first, select)


def assemble(own, received, mapping):
    width = mapping.shape[0]
    select = (mapping[:, None] == lax.broadcasted_iota(jnp.int32, (width, width), 1)).astype(
        jnp.bfloat16
    )
    stiff_nb = reorder_both(received[0], select)
    mass_nb = reorder_both(received[1], select)
    coup_nb = by_rows_t(received[2], select).astype(jnp.bfloat16)
    stiff_sum = (own[0].astype(jnp.float32) + stiff_nb).astype(jnp.bfloat16)
    mass_sum = (own[1].astype(jnp.float32) + mass_nb).astype(jnp.bfloat16)
    return (stiff_sum, mass_sum, jnp.concatenate([own[2], coup_nb], axis=0))


def send_blocks(axis, blocks):
    if axis == 0:
        return shifted((blocks[0], blocks[1], blocks[2]), "gx", -1)
    if axis == 1:
        return shifted((blocks[0], blocks[1], blocks[2]), "gy", -1)
    return shifted((blocks[0], blocks[1], blocks[2]), "gz", -1)


def local(constraint, stiff_ib, mass_ib, mass_ii, modes, stiff_faces, mass_faces, dof_map):
    constraint = constraint[0, 0, 0]
    stiff_ib = stiff_ib[0, 0, 0]
    mass_ib = mass_ib[0, 0, 0]
    mass_ii = mass_ii[0, 0, 0]
    modes = modes[0, 0, 0]
    stiff_faces = stiff_faces[0, 0, 0]
    mass_faces = mass_faces[0, 0, 0]
    dof_map = dof_map[0, 0, 0]
    loaded = (
        mass_ib.astype(jnp.float32) + mass_ii[:, None] * constraint.astype(jnp.float32)
    ).astype(jnp.bfloat16)
    common = (stiff_ib, mass_ib, constraint, loaded, modes, stiff_faces, mass_faces)
    results = []
    for axis in range(3):
        low_pieces = face_columns(2 * axis, *common)
        received = send_blocks(axis, reduce_face(*low_pieces))
        high_blocks = reduce_face(*face_columns(2 * axis + 1, *common))
        results.append(assemble(high_blocks, received, dof_map[axis]))
    stiff_out = jnp.stack([r[0] for r in results])[None, None, None]
    mass_out = jnp.stack([r[1] for r in results])[None, None, None]
    coup_out = jnp.stack([r[2] for r in results])[None, None, None]
    return (stiff_out, mass_out, coup_out)


def solution(mesh):
    placed = (
        P("gx", "gy", "gz", None, None),
        P("gx", "gy", "gz", None, None),
        P("gx", "gy", "gz", None, None),
        P("gx", "gy", "gz", None),
        P("gx", "gy", "gz", None, None),
        P("gx", "gy", "gz", None, None, None),
        P("gx", "gy", "gz", None, None),
        P("gx", "gy", "gz", None, None),
    )
    return jax.shard_map(
        local,
        mesh=mesh,
        in_specs=placed,
        out_specs=(
            P("gx", "gy", "gz", None, None, None),
            P("gx", "gy", "gz", None, None, None),
            P("gx", "gy", "gz", None, None, None),
        ),
        check_vma=False,
    )
```

profile of v0, /device:TPU:111, one launch (start us, length us, event | category | flops | bytes accessed | tf_op | source)
XLA Modules:
  0.0 92.6 jit_solution(9815226356834341858)
XLA Ops:
  0.6 0.9 %slice_convert_fusion.4 = (f32[1,1,1,1,512]{4,3,2,1,0:T(1,128)S(1)}, f32[1,1,1,1,512]{4,3,2,1,0:T(1,128)S(1)}, f32[1,1,1,1,512]{4,3,2,1,0:T(1,128)S(1)}, f32[1,1...) fusion(bf16[1,1,1,6,512]{4,3,2,1,0:T(8,128)(2,1)} %param.14), kind=kLoop, calls=%fused_computation.159 | loop fusion | flops 3072 | bytes 18432 | tf_op jit(solution)/shard_map/convert_element_type | solution.py:30
  1.6 2.8 %add_convert_fusion = bf16[256,3072]{1,0:T(8,128)(2,1)S(1)} fusion(f32[256]{0:T(256)} %bitcast.190, bf16[1,1,1,256,3072]{4,3,2,1,0:T(8,128)(2,1)} %param.10, bf16[1,1,1,256,3072]{4,3,2,1,0:T(8,128)(2,1)} %param.8), kind=kLoop, calls=%fused_computation | loop fusion | flops 3932160 | bytes 4719616 | tf_op jit(solution)/shard_map/convert_element_type | solution.py:89
  5.1 2.6 %collective-permute-start.5 = (bf16[512,512]{0,1:T(8,128)(2,1)S(1)}, bf16[512,512]{0,1:T(8,128)(2,1)}, u32[]{:S(2)}, u32[]{:S(2)}) collective-permute-start(bf16[512,512]{0,1:T(8,128)(2,1)S(1)} %fusion.21), channel_id=1, source_target_pairs={{1,0},{2,1},{3,2},{5,4},{6,5},{7,6},{9,8},{10,9},{11,10},{13,12},{... | collective-permute-start | bytes 1572872 | tf_op jit(solution)/shard_map/ppermute | solution.py:10
  8.0 1.2 %fusion.23 = bf16[512,512]{0,1:T(8,128)(2,1)} fusion(f32[512,512]{0,1:T(8,128)S(1)} %fusion.67, f32[512]{0:T(512)S(1)} %bitcast.179, bf16[256,3072]{1,0:T(8,128)(2,1)S(1)} %add_convert_fusion, bf16[256,3072]{1,0:T(8,128)(2,1)S(1)} %bitcast.148), kind=kOutput, calls=%fused_computation.51 | convolution fusion | flops 135528448 | bytes 2099200 | tf_op jit(solution)/shard_map/dot_general | solution.py:14
  9.2 3.3 %collective-permute-start.4 = (bf16[512,512]{0,1:T(8,128)(2,1)}, bf16[512,512]{0,1:T(8,128)(2,1)}, u32[]{:S(2)}, u32[]{:S(2)}) collective-permute-start(bf16[512,512]{0,1:T(8,128)(2,1)} %fusion.23), channel_id=1, source_target_pairs={{4,0},{8,4},{12,8},{16,12},{20,16},{24,20},{28,24},{5,1},{9,5},{13... | collective-permute-start | bytes 1572872 | tf_op jit(solution)/shard_map/ppermute | solution.py:10
  12.8 1.1 %fusion.25 = bf16[512,512]{0,1:T(8,128)(2,1)} fusion(f32[512,512]{0,1:T(8,128)S(1)} %fusion.71, f32[512]{0:T(512)S(1)} %bitcast.178, bf16[256,3072]{1,0:T(8,128)(2,1)S(1)} %add_convert_fusion, bf16[256,3072]{1,0:T(8,128)(2,1)S(1)} %bitcast.150), kind=kOutput, calls=%fused_computation.53 | convolution fusion | flops 135528448 | bytes 2099200 | tf_op jit(solution)/shard_map/dot_general | solution.py:14
  13.9 1.9 %collective-permute-start.3 = (bf16[512,512]{0,1:T(8,128)(2,1)}, bf16[512,512]{0,1:T(8,128)(2,1)}, u32[]{:S(2)}, u32[]{:S(2)}) collective-permute-start(bf16[512,512]{0,1:T(8,128)(2,1)} %fusion.25), channel_id=1, source_target_pairs={{32,0},{64,32},{96,64},{128,96},{160,128},{192,160},{224,192},{33,... | collective-permute-start | bytes 1572872 | tf_op jit(solution)/shard_map/ppermute | solution.py:10
  16.2 1.9 %collective-permute-start.6 = (bf16[300,512]{0,1:T(8,128)(2,1)S(1)}, bf16[300,512]{0,1:T(8,128)(2,1)S(1)}, u32[]{:S(2)}, u32[]{:S(2)}) collective-permute-start(bf16[300,512]{0,1:T(8,128)(2,1)S(1)} %fusion.42), channel_id=1, source_target_pairs={{32,0},{64,32},{96,64},{128,96},{160,128},{192,160},{224,192},{33,... | collective-permute-start | bytes 921608 | tf_op jit(solution)/shard_map/ppermute | solution.py:10
  18.5 1.4 %collective-permute-start.7 = (bf16[300,512]{0,1:T(8,128)(2,1)S(1)}, bf16[300,512]{0,1:T(8,128)(2,1)S(1)}, u32[]{:S(2)}, u32[]{:S(2)}) collective-permute-start(bf16[300,512]{0,1:T(8,128)(2,1)S(1)} %fusion.43), channel_id=1, source_target_pairs={{4,0},{8,4},{12,8},{16,12},{20,16},{24,20},{28,24},{5,1},{9,5},{13... | collective-permute-start | bytes 921608 | tf_op jit(solution)/shard_map/ppermute | solution.py:10
  21.3 1.0 %copy-done.4 = bf16[1,1,1,6,512,512]{5,4,3,2,1,0:T(8,128)(2,1)S(1)} copy-done((bf16[1,1,1,6,512,512]{5,4,3,2,1,0:T(8,128)(2,1)S(1)}, bf16[1,1,1,6,512,512]{5,4,3,2,1,0:T(8,128)(2,1)}, u32[]{:S(2)}) %copy-start.4) | copy-done | bytes 3145752
  22.3 1.1 %fusion.20 = bf16[512,512]{1,0:T(8,128)(2,1)} fusion(bf16[1,1,1,6,512,512]{5,4,3,2,1,0:T(8,128)(2,1)S(1)} %copy-done.4, bf16[256,3072]{1,0:T(8,128)(2,1)S(1)} %bitcast.169, bf16[256,3072]{1,0:T(8,128)(2,1)S(1)} %bitcast.154), kind=kOutput, calls=%fused_computation.48 | convolution fusion | flops 135004160 | bytes 1572864 | tf_op jit(solution)/shard_map/dot_general | solution.py:14
  23.5 1.3 %fusion.19 = f32[512,512]{1,0:T(8,128)} fusion(bf16[1,1,1,6,512,512]{5,4,3,2,1,0:T(8,128)(2,1)S(1)} %copy-done.4, bf16[256,3072]{1,0:T(8,128)(2,1)S(1)} %bitcast.170, bf16[256,3072]{1,0:T(8,128)(2,1)S(1)} %bitcast.155), kind=kOutput, calls=%fused_computation.47 | convolution fusion | flops 135266304 | bytes 2097152 | tf_op jit(solution)/shard_map/dot_general | solution.py:14
  24.8 1.2 %fusion.17 = bf16[512,512]{1,0:T(8,128)(2,1)} fusion(bf16[1,1,1,6,512,512]{5,4,3,2,1,0:T(8,128)(2,1)S(1)} %copy-done.4, bf16[256,3072]{1,0:T(8,128)(2,1)S(1)} %bitcast.171, bf16[256,3072]{1,0:T(8,128)(2,1)S(1)} %bitcast.156), kind=kOutput, calls=%fused_computation.45 | convolution fusion | flops 135004160 | bytes 1572864 | tf_op jit(solution)/shard_map/dot_general | solution.py:14
  26.0 1.3 %fusion.16 = f32[512,512]{1,0:T(8,128)} fusion(bf16[1,1,1,6,512,512]{5,4,3,2,1,0:T(8,128)(2,1)S(1)} %copy-done.4, bf16[256,3072]{1,0:T(8,128)(2,1)S(1)} %bitcast.172, bf16[256,3072]{1,0:T(8,128)(2,1)S(1)} %bitcast.157), kind=kOutput, calls=%fused_computation.44 | convolution fusion | flops 135266304 | bytes 2097152 | tf_op jit(solution)/shard_map/dot_general | solution.py:14
  27.3 1.2 %fusion.14 = bf16[512,512]{1,0:T(8,128)(2,1)} fusion(bf16[1,1,1,6,512,512]{5,4,3,2,1,0:T(8,128)(2,1)S(1)} %copy-done.4, bf16[256,3072]{1,0:T(8,128)(2,1)S(1)} %bitcast.173, bf16[256,3072]{1,0:T(8,128)(2,1)S(1)} %bitcast.158), kind=kOutput, calls=%fused_computation.42 | convolution fusion | flops 135004160 | bytes 1572864 | tf_op jit(solution)/shard_map/dot_general | solution.py:14
  29.6 1.3 %fusion.29 = f32[512,512]{0,1:T(8,128)} fusion(f32[512,512]{0,1:T(8,128)S(1)} %fusion.65, f32[512]{0:T(512)S(1)} %bitcast.177, bf16[256,3072]{1,0:T(8,128)(2,1)S(1)} %add_convert_fusion, bf16[256,3072]{1,0:T(8,128)(2,1)S(1)} %bitcast.160), kind=kOutput, calls=%fused_computation.57 | convolution fusion | flops 135790592 | bytes 2623488 | tf_op jit(solution)/shard_map/dot_general | solution.py:14
  32.0 7.7 %collective-permute-done.6 = bf16[300,512]{0,1:T(8,128)(2,1)S(1)} collective-permute-done((bf16[300,512]{0,1:T(8,128)(2,1)S(1)}, bf16[300,512]{0,1:T(8,128)(2,1)S(1)}, u32[]{:S(2)}, u32[]{:S(2)}) %collective-permute-start.6) | collective-permute-done | bytes 307232 | tf_op jit(solution)/shard_map/ppermute | solution.py:10
  39.7 2.3 %collective-permute-start.2 = (bf16[512,512]{1,0:T(8,128)(2,1)}, bf16[512,512]{1,0:T(8,128)(2,1)}, u32[]{:S(2)}, u32[]{:S(2)}) collective-permute-start(bf16[512,512]{1,0:T(8,128)(2,1)} %fusion.20), channel_id=1, source_target_pairs={{1,0},{2,1},{3,2},{5,4},{6,5},{7,6},{9,8},{10,9},{11,10},{13,12},{... | collective-permute-start | bytes 1572872 | tf_op jit(solution)/shard_map/ppermute | solution.py:10
  42.5 1.9 %collective-permute-start.8 = (bf16[300,512]{0,1:T(8,128)(2,1)S(1)}, bf16[300,512]{0,1:T(8,128)(2,1)S(1)}, u32[]{:S(2)}, u32[]{:S(2)}) collective-permute-start(bf16[300,512]{0,1:T(8,128)(2,1)S(1)} %fusion.44), channel_id=1, source_target_pairs={{1,0},{2,1},{3,2},{5,4},{6,5},{7,6},{9,8},{10,9},{11,10},{13,12},{... | collective-permute-start | bytes 921608 | tf_op jit(solution)/shard_map/ppermute | solution.py:10
  45.1 22.2 %collective-permute-done.8 = bf16[300,512]{0,1:T(8,128)(2,1)S(1)} collective-permute-done((bf16[300,512]{0,1:T(8,128)(2,1)S(1)}, bf16[300,512]{0,1:T(8,128)(2,1)S(1)}, u32[]{:S(2)}, u32[]{:S(2)}) %collective-permute-start.8) | collective-permute-done | bytes 307232 | tf_op jit(solution)/shard_map/ppermute | solution.py:10
  67.3 2.1 %collective-permute-start.1 = (bf16[512,512]{1,0:T(8,128)(2,1)}, bf16[512,512]{1,0:T(8,128)(2,1)}, u32[]{:S(2)}, u32[]{:S(2)}) collective-permute-start(bf16[512,512]{1,0:T(8,128)(2,1)} %fusion.17), channel_id=1, source_target_pairs={{4,0},{8,4},{12,8},{16,12},{20,16},{24,20},{28,24},{5,1},{9,5},{13... | collective-permute-start | bytes 1572872 | tf_op jit(solution)/shard_map/ppermute | solution.py:10
  70.0 1.4 %maximum_bitcast_fusion = bf16[1,1,1,3,600,512]{5,4,3,2,1,0:T(8,128)(2,1)} fusion(bf16[1,600,512]{2,1,0:T(8,128)(2,1)S(1)} %maximum_bitcast_fusion.5, bf16[1,600,512]{2,1,0:T(8,128)(2,1)S(1)} %maximum_bitcast_fusion.4, bf16[1,600,512]{2,1,0:T(8,128)(2,1)S(1)} %maximum_bitcast_fusion.3), kind=kLoop, calls=%fused_computation.1 | loop fusion | flops 1843200 | bytes 3686400 | tf_op jit(solution)/shard_map/broadcast_in_dim | solution.py:99
  71.4 2.1 %collective-permute-start = (bf16[512,512]{1,0:T(8,128)(2,1)}, bf16[512,512]{1,0:T(8,128)(2,1)}, u32[]{:S(2)}, u32[]{:S(2)}) collective-permute-start(bf16[512,512]{1,0:T(8,128)(2,1)} %fusion.14), channel_id=1, source_target_pairs={{32,0},{64,32},{96,64},{128,96},{160,128},{192,160},{224,192},{33,... | collective-permute-start | bytes 1572872 | tf_op jit(solution)/shard_map/ppermute | solution.py:10
  73.5 3.1 %fusion.36 = bf16[1,512,512]{1,2,0:T(8,128)(2,1)} fusion(f32[512,512]{0,1:T(8,128)} %fusion.29, bf16[512,512]{0,1:T(8,128)(2,1)} %collective-permute-done.5, s32[512]{0:T(512)S(1)} %bitcast.188), kind=kOutput, calls=%fused_computation.67 | convolution fusion | flops 538181632 | bytes 2099200 | tf_op jit(solution)/shard_map/dot_general | solution.py:20
  76.6 2.7 %fusion.37 = bf16[1,512,512]{1,2,0:T(8,128)(2,1)} fusion(f32[512,512]{0,1:T(8,128)S(1)} %fusion.28, bf16[512,512]{0,1:T(8,128)(2,1)} %collective-permute-done.4, s32[512]{0:T(512)S(1)} %bitcast.185), kind=kOutput, calls=%fused_computation.68 | convolution fusion | flops 538181632 | bytes 2099200 | tf_op jit(solution)/shard_map/dot_general | solution.py:20
  79.3 2.7 %fusion.38 = bf16[1,512,512]{1,2,0:T(8,128)(2,1)} fusion(f32[512,512]{0,1:T(8,128)S(1)} %fusion.27, bf16[512,512]{0,1:T(8,128)(2,1)} %collective-permute-done.3, s32[512]{0:T(512)S(1)} %bitcast.182), kind=kOutput, calls=%fused_computation.69 | convolution fusion | flops 538181632 | bytes 2099200 | tf_op jit(solution)/shard_map/dot_general | solution.py:20
  82.0 1.5 %maximum_bitcast_fusion.2 = bf16[1,1,1,3,512,512]{4,5,3,2,1,0:T(8,128)(2,1)S(1)} fusion(bf16[1,512,512]{1,2,0:T(8,128)(2,1)} %fusion.36, bf16[1,512,512]{1,2,0:T(8,128)(2,1)} %fusion.37, bf16[1,512,512]{1,2,0:T(8,128)(2,1)} %fusion.38), kind=kLoop, calls=%fused_computation.3 | loop fusion | flops 1572864 | bytes 3145728 | tf_op jit(solution)/shard_map/broadcast_in_dim | solution.py:98
  83.6 1.6 %copy.17 = bf16[1,1,1,3,512,512]{5,4,3,2,1,0:T(8,128)(2,1)} copy(bf16[1,1,1,3,512,512]{4,5,3,2,1,0:T(8,128)(2,1)S(1)} %maximum_bitcast_fusion.2) | data formatting | bytes 3145728
  85.2 2.3 %fusion.39 = bf16[1,512,512]{2,1,0:T(8,128)(2,1)S(1)} fusion(f32[512,512]{1,0:T(8,128)} %fusion.19, bf16[512,512]{1,0:T(8,128)(2,1)} %collective-permute-done.2, s32[512]{0:T(512)S(1)} %bitcast.189), kind=kOutput, calls=%fused_computation.70 | convolution fusion | flops 538181632 | bytes 2099200 | tf_op jit(solution)/shard_map/dot_general | solution.py:20
  87.5 1.9 %fusion.40 = bf16[1,512,512]{2,1,0:T(8,128)(2,1)S(1)} fusion(f32[512,512]{1,0:T(8,128)S(1)} %copy-done.3, bf16[512,512]{1,0:T(8,128)(2,1)} %collective-permute-done.1, s32[512]{0:T(512)S(1)} %bitcast.186), kind=kOutput, calls=%fused_computation.71 | convolution fusion | flops 538181632 | bytes 2099200 | tf_op jit(solution)/shard_map/dot_general | solution.py:20
  89.4 1.9 %fusion.41 = bf16[1,512,512]{2,1,0:T(8,128)(2,1)S(1)} fusion(f32[512,512]{1,0:T(8,128)S(1)} %fusion.13, bf16[512,512]{1,0:T(8,128)(2,1)} %collective-permute-done, s32[512]{0:T(512)S(1)} %bitcast.183), kind=kOutput, calls=%fused_computation.72 | convolution fusion | flops 538181632 | bytes 2099200 | tf_op jit(solution)/shard_map/dot_general | solution.py:20
  91.3 1.3 %maximum_bitcast_fusion.1 = bf16[1,1,1,3,512,512]{5,4,3,2,1,0:T(8,128)(2,1)} fusion(bf16[1,512,512]{2,1,0:T(8,128)(2,1)S(1)} %fusion.39, bf16[1,512,512]{2,1,0:T(8,128)(2,1)S(1)} %fusion.40, bf16[1,512,512]{2,1,0:T(8,128)(2,1)S(1)} %fusion.41), kind=kLoop, calls=%fused_computation.2 | loop fusion | flops 1572864 | bytes 3145728 | tf_op jit(solution)/shard_map/broadcast_in_dim | solution.py:97
  (43 shorter events, 7.4 us)
Async XLA Ops:
  0.6 15.2 %copy-start = (bf16[1,1,1,300,256]{4,3,2,1,0:T(8,128)(2,1)S(1)}, bf16[1,1,1,300,256]{4,3,2,1,0:T(8,128)(2,1)}, u32[]{:S(2)}) copy-start(bf16[1,1,1,300,256]{4,3,2,1,0:T(8,128)(2,1)} %param.12) | copy-start | bytes 460804
  1.6 2.8 %copy-start.1 = (bf16[1,1,1,256,3072]{4,3,2,1,0:T(8,128)(2,1)S(1)}, bf16[1,1,1,256,3072]{4,3,2,1,0:T(8,128)(2,1)}, u32[]{:S(2)}) copy-start(bf16[1,1,1,256,3072]{4,3,2,1,0:T(8,128)(2,1)} %param.8) | copy-start | bytes 4718596
  1.6 2.8 %copy-start.2 = (bf16[1,1,1,256,3072]{4,3,2,1,0:T(8,128)(2,1)S(1)}, bf16[1,1,1,256,3072]{4,3,2,1,0:T(8,128)(2,1)}, u32[]{:S(2)}) copy-start(bf16[1,1,1,256,3072]{4,3,2,1,0:T(8,128)(2,1)} %param.10) | copy-start | bytes 4718596
  5.1 66.3 %collective-permute-start.5 = (bf16[512,512]{0,1:T(8,128)(2,1)S(1)}, bf16[512,512]{0,1:T(8,128)(2,1)}, u32[]{:S(2)}, u32[]{:S(2)}) collective-permute-start(bf16[512,512]{0,1:T(8,128)(2,1)S(1)} %fusion.21), channel_id=1, source_target_pairs={{1,0},{2,1},{3,2},{5,4},{6,5},{7,6},{9,8},{10,9},{11,10},{13,12},{... | collective-permute-start | bytes 1572872 | tf_op jit(solution)/shard_map/ppermute | solution.py:10
  9.2 67.4 %collective-permute-start.4 = (bf16[512,512]{0,1:T(8,128)(2,1)}, bf16[512,512]{0,1:T(8,128)(2,1)}, u32[]{:S(2)}, u32[]{:S(2)}) collective-permute-start(bf16[512,512]{0,1:T(8,128)(2,1)} %fusion.23), channel_id=1, source_target_pairs={{4,0},{8,4},{12,8},{16,12},{20,16},{24,20},{28,24},{5,1},{9,5},{13... | collective-permute-start | bytes 1572872 | tf_op jit(solution)/shard_map/ppermute | solution.py:10
  13.9 65.4 %collective-permute-start.3 = (bf16[512,512]{0,1:T(8,128)(2,1)}, bf16[512,512]{0,1:T(8,128)(2,1)}, u32[]{:S(2)}, u32[]{:S(2)}) collective-permute-start(bf16[512,512]{0,1:T(8,128)(2,1)} %fusion.25), channel_id=1, source_target_pairs={{32,0},{64,32},{96,64},{128,96},{160,128},{192,160},{224,192},{33,... | collective-permute-start | bytes 1572872 | tf_op jit(solution)/shard_map/ppermute | solution.py:10
  16.2 23.4 %collective-permute-start.6 = (bf16[300,512]{0,1:T(8,128)(2,1)S(1)}, bf16[300,512]{0,1:T(8,128)(2,1)S(1)}, u32[]{:S(2)}, u32[]{:S(2)}) collective-permute-start(bf16[300,512]{0,1:T(8,128)(2,1)S(1)} %fusion.42), channel_id=1, source_target_pairs={{32,0},{64,32},{96,64},{128,96},{160,128},{192,160},{224,192},{33,... | collective-permute-start | bytes 921608 | tf_op jit(solution)/shard_map/ppermute | solution.py:10
  18.5 24.0 %collective-permute-start.7 = (bf16[300,512]{0,1:T(8,128)(2,1)S(1)}, bf16[300,512]{0,1:T(8,128)(2,1)S(1)}, u32[]{:S(2)}, u32[]{:S(2)}) collective-permute-start(bf16[300,512]{0,1:T(8,128)(2,1)S(1)} %fusion.43), channel_id=1, source_target_pairs={{4,0},{8,4},{12,8},{16,12},{20,16},{24,20},{28,24},{5,1},{9,5},{13... | collective-permute-start | bytes 921608 | tf_op jit(solution)/shard_map/ppermute | solution.py:10
  19.9 1.4 %copy-start.5 = (bf16[1,1,1,256,3072]{4,3,2,1,0:T(8,128)(2,1)S(1)}, bf16[1,1,1,256,3072]{4,3,2,1,0:T(8,128)(2,1)}, u32[]{:S(2)}) copy-start(bf16[1,1,1,256,3072]{4,3,2,1,0:T(8,128)(2,1)} %param.9) | copy-start | bytes 4718596
  20.2 2.1 %copy-start.4 = (bf16[1,1,1,6,512,512]{5,4,3,2,1,0:T(8,128)(2,1)S(1)}, bf16[1,1,1,6,512,512]{5,4,3,2,1,0:T(8,128)(2,1)}, u32[]{:S(2)}) copy-start(bf16[1,1,1,6,512,512]{5,4,3,2,1,0:T(8,128)(2,1)} %param.13) | copy-start | bytes 9437188
  31.3 0.7 copy-start.6
  39.7 45.5 %collective-permute-start.2 = (bf16[512,512]{1,0:T(8,128)(2,1)}, bf16[512,512]{1,0:T(8,128)(2,1)}, u32[]{:S(2)}, u32[]{:S(2)}) collective-permute-start(bf16[512,512]{1,0:T(8,128)(2,1)} %fusion.20), channel_id=1, source_target_pairs={{1,0},{2,1},{3,2},{5,4},{6,5},{7,6},{9,8},{10,9},{11,10},{13,12},{... | collective-permute-start | bytes 1572872 | tf_op jit(solution)/shard_map/ppermute | solution.py:10
  42.5 24.8 %collective-permute-start.8 = (bf16[300,512]{0,1:T(8,128)(2,1)S(1)}, bf16[300,512]{0,1:T(8,128)(2,1)S(1)}, u32[]{:S(2)}, u32[]{:S(2)}) collective-permute-start(bf16[300,512]{0,1:T(8,128)(2,1)S(1)} %fusion.44), channel_id=1, source_target_pairs={{1,0},{2,1},{3,2},{5,4},{6,5},{7,6},{9,8},{10,9},{11,10},{13,12},{... | collective-permute-start | bytes 921608 | tf_op jit(solution)/shard_map/ppermute | solution.py:10
  67.3 20.1 %collective-permute-start.1 = (bf16[512,512]{1,0:T(8,128)(2,1)}, bf16[512,512]{1,0:T(8,128)(2,1)}, u32[]{:S(2)}, u32[]{:S(2)}) collective-permute-start(bf16[512,512]{1,0:T(8,128)(2,1)} %fusion.17), channel_id=1, source_target_pairs={{4,0},{8,4},{12,8},{16,12},{20,16},{24,20},{28,24},{5,1},{9,5},{13... | collective-permute-start | bytes 1572872 | tf_op jit(solution)/shard_map/ppermute | solution.py:10
  71.4 17.9 %collective-permute-start = (bf16[512,512]{1,0:T(8,128)(2,1)}, bf16[512,512]{1,0:T(8,128)(2,1)}, u32[]{:S(2)}, u32[]{:S(2)}) collective-permute-start(bf16[512,512]{1,0:T(8,128)(2,1)} %fusion.14), channel_id=1, source_target_pairs={{32,0},{64,32},{96,64},{128,96},{160,128},{192,160},{224,192},{33,... | collective-permute-start | bytes 1572872 | tf_op jit(solution)/shard_map/ppermute | solution.py:10
  85.1 2.3 %copy-start.3 = (f32[512,512]{1,0:T(8,128)S(1)}, f32[512,512]{1,0:T(8,128)}, u32[]{:S(2)}) copy-start(f32[512,512]{1,0:T(8,128)} %fusion.16) | copy-start | bytes 3145732
where the time goes:
time: 93.3 us; the launch traced here: 92.6 us
  matrix products  30.9 us (33%)
  waiting for transfers between devices  29.9 us (32%)
  starting transfers between devices  19.4 us (21%)
  other arithmetic  8.24 us (9%)
  local copies, waits for them, and re-layouts  3.12 us (3%)
  between operations  0.97 us (1%)
    ppermute x9, waiting for transfers between devices, shifted(): return lax.ppermute(block, axis, route)  29.9 us
    ppermute x9, starting transfers between devices, shifted(): return lax.ppermute(block, axis, route)  19.4 us
    dot_general x9, matrix products, by_rows_t(): lax.dot_general(left, right, (((1,), (1,)), ((), ())), preferred_element_...  16.1 us
    dot_general x18, matrix products, transposed(): lax.dot_general(left, right, (((0,), (0,)), ((), ())), preferred_element_...  13 us
    unnamed x15, local copies, waits for them, and re-layouts  3.11 us
    convert_element_type x1, other arithmetic, local(): loaded = (mass_ib.astype(jnp.float32) + mass_ii[:, None] * constraint.ast...  2.79 us
  transfers between devices with their start and end apart: 9, of which 2 were waited for; matrix products, arithmetic and copies ran while one was open for 36% of the time, Pallas kernels for 0%

commit v1 on v0

v1 whole, which is shorter than its diff:
```python
import functools

import jax
import jax.numpy as jnp
from jax import lax
from jax.experimental import pallas as pl
from jax.experimental.pallas import tpu as pltpu
from jax.sharding import PartitionSpec as P

MESH = pl.DeviceIdType.MESH
AXES = ("gx", "gy", "gz")
BF16 = jnp.bfloat16
F32 = jnp.float32


def turned(left, right):
    return lax.dot_general(left, right, (((0,), (0,)), ((), ())), preferred_element_type=F32)


def times(left, right):
    return jnp.dot(left, right, preferred_element_type=F32)


def column_of(row, lanes=128):
    return jnp.broadcast_to(row, (lanes, row.shape[1])).T


def exchange(
    sizes,
    parts,
    cons_in,
    stiff_in,
    mass_in,
    mii_in,
    modes_in,
    faces_in,
    mfaces_in,
    dof_in,
    stiff_out,
    mass_out,
    coup_out,
    cons,
    stiff,
    mass,
    mii,
    modes,
    faces,
    mfaces,
    dof,
    lump,
    load,
    select,
    select_t,
    dcol,
    full,
    half,
    stiff_send,
    mass_send,
    diag_send,
    coup_send,
    stiff_recv,
    mass_recv,
    diag_recv,
    coup_recv,
    col_sem,
    face_sem,
    small_sem,
    stiff_sems,
    mass_sems,
    diag_sems,
    coup_sems,
):
    width = faces.shape[-1]
    mid = width // 2
    n_modes = modes.shape[0]
    here = [lax.axis_index(name) for name in AXES]
    lower = [h > 0 for h in here]
    upper = [h < n - 1 for h, n in zip(here, sizes, strict=True)]
    upper_flag = [jnp.where(u, 1, 0) for u in upper]

    def has_upper(axis):
        x, y, z = upper_flag
        return (x * ((1 - axis) * (2 - axis) // 2) + y * (axis * (2 - axis)) + z * (axis * (axis - 1) // 2)) > 0

    def columns(which, array, scratch, face):
        return pltpu.make_async_copy(
            array.at[:, pl.ds(face * width, width)], scratch.at[face], col_sem.at[which, face]
        )

    def face_block(face):
        return pltpu.make_async_copy(faces_in.at[face], faces.at[face], face_sem.at[face])

    small = [
        pltpu.make_async_copy(source, target, small_sem.at[k])
        for k, (source, target) in enumerate(
            ((mii_in, mii), (modes_in, modes), (mfaces_in, mfaces), (dof_in, dof))
        )
    ]
    for face in (0, 2, 4):
        columns(0, cons_in, cons, face).start()
        columns(1, stiff_in, stiff, face).start()
        face_block(face).start()
    for copy in small:
        copy.start()
    for face in (0, 2, 4):
        columns(2, mass_in, mass, face).start()
    for face in (1, 3, 5):
        columns(0, cons_in, cons, face).start()
        columns(1, stiff_in, stiff, face).start()
        columns(2, mass_in, mass, face).start()
        face_block(face).start()

    barrier = pltpu.get_barrier_semaphore()
    for axis in range(3):

        @pl.when(upper[axis])
        def _(axis=axis):
            pl.semaphore_signal(
                barrier, inc=1, device_id={AXES[axis]: here[axis] + 1}, device_id_type=MESH
            )

    def remote(axis, name, source, target, sems, index):
        return pltpu.make_async_remote_copy(
            src_ref=source,
            dst_ref=target,
            send_sem=sems.at[(0, *index)],
            recv_sem=sems.at[(1, *index)],
            device_id={name: here[AXES.index(name)] - 1},
            device_id_type=MESH,
        )

    def stiff_copy(axis, name="gx"):
        return remote(axis, name, stiff_send.at[axis], stiff_recv.at[axis], stiff_sems, (axis,))

    def mass_copy(axis, name="gx"):
        return remote(axis, name, mass_send.at[axis], mass_recv.at[axis], mass_sems, (axis,))

    def diag_copy(axis, name="gx"):
        return remote(axis, name, diag_send.at[axis], diag_recv.at[axis], diag_sems, (axis,))

    def coup_copy(axis, part, name="gx"):
        rows = pl.ds(*parts[part])
        return remote(
            axis, name, coup_send.at[axis, rows], coup_recv.at[axis, rows], coup_sems, (axis, part)
        )

    for axis in range(3):
        face = 2 * axis
        columns(0, cons_in, cons, face).wait()
        columns(1, stiff_in, stiff, face).wait()
        face_block(face).wait()
        stiff_send[axis] = (turned(stiff[face], cons[face]) + faces[face].astype(F32)).astype(BF16)
        if axis == 0:
            peers = sum(jnp.where(low, 1, 0) for low in lower)

            @pl.when(peers > 0)
            def _():
                pl.semaphore_wait(barrier, peers)

        @pl.when(lower[axis])
        def _(axis=axis):
            stiff_copy(axis, AXES[axis]).start()

    for copy in small:
        copy.wait()
    dcol[...] = column_of(mii[...])
    for face in range(6):
        lump[face] = mfaces[pl.ds(face, 1), :].astype(F32)

    def loaded(face):
        scale = jnp.tile(dcol[...], (1, width // 128))
        load[face] = (mass[face].astype(F32) + scale * cons[face].astype(F32)).astype(BF16)

    row = lax.broadcasted_iota(jnp.int32, (mid, mid), 0)
    column = lax.broadcasted_iota(jnp.int32, (mid, mid), 1)
    left, right = pl.ds(0, mid), pl.ds(mid, mid)
    for axis in range(3):
        face = 2 * axis
        columns(2, mass_in, mass, face).wait()
        loaded(face)

        def block(rows, cols, face=face):
            return turned(cons[face, :, rows], load[face, :, cols]) + turned(
                mass[face, :, rows], cons[face, :, cols]
            )

        lumped = lump[face]
        high_block = block(right, right) + jnp.where(row == column, lumped[:, mid:], 0.0)
        diagonal = jnp.sum(jnp.where(row == column, high_block, 0.0), axis=0, keepdims=True)
        diag_send[axis] = jnp.broadcast_to(diagonal, diag_send.shape[1:]).astype(BF16)
        low_block = block(left, left) + jnp.where(row == column, lumped[:, :mid], 0.0)
        mass_send[axis, :, right] = jnp.where(row <= column, low_block, high_block).astype(BF16)
        mass_send[axis, :, left] = block(left, right).astype(BF16)

        @pl.when(lower[axis])
        def _(axis=axis):
            diag_copy(axis, AXES[axis]).start()
            mass_copy(axis, AXES[axis]).start()

    for axis in range(3):
        coup_send[axis, pl.ds(coup_send.shape[1] - 8, 8), :] = jnp.zeros((8, width), BF16)
        coup_send[axis, pl.ds(0, n_modes), :] = times(modes[...], load[2 * axis]).astype(BF16)

        @pl.when(lower[axis])
        def _(axis=axis):
            for part in range(len(parts)):
                coup_copy(axis, part, AXES[axis]).start()

    for axis in range(3):

        @pl.when(jnp.logical_not(upper[axis]))
        def _(axis=axis):
            stiff_recv[axis] = jnp.zeros(stiff_recv.shape[1:], BF16)
            mass_recv[axis] = jnp.zeros(mass_recv.shape[1:], BF16)
            diag_recv[axis] = jnp.zeros(diag_recv.shape[1:], BF16)
            coup_recv[axis] = jnp.zeros(coup_recv.shape[1:], BF16)

    for face in (1, 3, 5):
        columns(0, cons_in, cons, face).wait()
        columns(1, stiff_in, stiff, face).wait()
        columns(2, mass_in, mass, face).wait()
        face_block(face).wait()

    def own(axis, carry):
        face = 2 * axis + 1
        loaded(face)
        stiff_out[axis] = (turned(stiff[face], cons[face]) + faces[face].astype(F32)).astype(BF16)
        wide_row = lax.broadcasted_iota(jnp.int32, (width, width), 0)
        wide_column = lax.broadcasted_iota(jnp.int32, (width, width), 1)
        lumped = lump[face]
        mass_out[axis] = (
            turned(cons[face], load[face])
            + turned(mass[face], cons[face])
            + jnp.where(wide_row == wide_column, lumped, 0.0)
        ).astype(BF16)
        coup_out[axis, pl.ds(0, n_modes), :] = times(modes[...], load[face]).astype(BF16)
        mapping = dof[axis]
        select[axis] = jnp.where(mapping == wide_row, 1.0, 0.0).astype(BF16)
        spread = jnp.tile(column_of(mapping.astype(F32)), (1, width // 128)).astype(jnp.int32)
        select_t[axis] = jnp.where(spread == wide_column, 1.0, 0.0).astype(BF16)
        return carry

    lax.fori_loop(0, 3, own, 0)

    def reorder(axis, source, out):
        half[...] = times(source, select[axis]).astype(BF16)
        out[axis] = (out[axis].astype(F32) + times(select_t[axis], half[...])).astype(BF16)

    def take_stiff(step, carry):
        axis = lax.rem(step + 2, 3)

        @pl.when(has_upper(axis))
        def _():
            stiff_copy(axis).wait_recv()

        reorder(axis, stiff_recv[axis], stiff_out)
        return carry

    lax.fori_loop(0, 3, take_stiff, 0)

    def take_mass(step, carry):
        axis = lax.rem(step + 2, 3)

        @pl.when(has_upper(axis))
        def _():
            diag_copy(axis).wait_recv()
            mass_copy(axis).wait_recv()

        packed = mass_recv[axis, :, right].astype(F32)
        flipped = packed.T
        across = mass_recv[axis, :, left]
        diagonal = diag_recv[axis].astype(F32)[0:1, :]
        full[left, left] = jnp.where(row <= column, packed, flipped).astype(BF16)
        full[right, right] = jnp.where(
            row > column, packed, jnp.where(row < column, flipped, diagonal)
        ).astype(BF16)
        full[left, right] = across
        full[right, left] = across.astype(F32).T.astype(BF16)
        reorder(axis, full[...], mass_out)
        return carry

    lax.fori_loop(0, 3, take_mass, 0)

    for part, (start, size) in enumerate(parts):

        def take_coup(step, carry, part=part, start=start, size=size):
            axis = lax.rem(step + 2, 3)

            @pl.when(has_upper(axis))
            def _():
                coup_copy(axis, part).wait_recv()

            kept = min(size, n_modes - start)
            moved = times(coup_recv[axis, pl.ds(start, size), :], select[axis]).astype(BF16)
            coup_out[axis, pl.ds(n_modes + start, kept), :] = moved[:kept]
            return carry

        lax.fori_loop(0, 3, take_coup, 0)

    for axis in range(3):

        @pl.when(lower[axis])
        def _(axis=axis):
            stiff_copy(axis).wait_send()
            diag_copy(axis).wait_send()
            mass_copy(axis).wait_send()
            for part in range(len(parts)):
                coup_copy(axis, part).wait_send()


def write_out(stiff_in, mass_in, coup_in, stiff_out, mass_out, coup_out, sems):
    copies = [
        pltpu.make_async_copy(source.at[axis], target.at[axis], sems.at[k, axis])
        for k, (source, target) in enumerate(
            ((stiff_in, stiff_out), (mass_in, mass_out), (coup_in, coup_out))
        )
        for axis in range(3)
    ]
    for copy in copies:
        copy.start()
    for copy in copies:
        copy.wait()


def local(sizes, constraint, stiff_ib, mass_ib, mass_ii, modes, stiff_faces, mass_faces, dof_map):
    depth = constraint.shape[-2]
    width = stiff_faces.shape[-1]
    n_modes = modes.shape[-2]
    mid = width // 2
    tall = -(-n_modes // 8) * 8
    quarter = -(-tall // 32) * 8
    parts = [(start, min(quarter, tall - start)) for start in range(0, tall, quarter)]
    shapes = ((3, width, width), (3, width, width), (3, 2 * n_modes, width))
    hbm = pl.BlockSpec(memory_space=pltpu.HBM)
    vmem = pl.BlockSpec(memory_space=pltpu.VMEM)
    dma = pltpu.SemaphoreType.DMA
    blocks = pl.pallas_call(
        functools.partial(exchange, sizes, parts),
        out_shape=[pltpu.VMEM(shape, BF16) for shape in shapes],
        in_specs=[hbm] * 8,
        out_specs=[vmem] * 3,
        scratch_shapes=[
            pltpu.VMEM((6, depth, width), BF16),
            pltpu.VMEM((6, depth, width), BF16),
            pltpu.VMEM((6, depth, width), BF16),
            pltpu.VMEM((1, depth), F32),
            pltpu.VMEM((n_modes, depth), BF16),
            pltpu.VMEM((6, width, width), BF16),
            pltpu.VMEM((6, width), BF16),
            pltpu.VMEM((3, 1, width), jnp.int32),
            pltpu.VMEM((6, 1, width), F32),
            pltpu.VMEM((6, depth, width), BF16),
            pltpu.VMEM((3, width, width), BF16),
            pltpu.VMEM((3, width, width), BF16),
            pltpu.VMEM((depth, 128), F32),
            pltpu.VMEM((width, width), BF16),
            pltpu.VMEM((width, width), BF16),
            pltpu.VMEM((3, width, width), BF16),
            pltpu.VMEM((3, mid, width), BF16),
            pltpu.VMEM((3, 16, mid), BF16),
            pltpu.VMEM((3, tall, width), BF16),
            pltpu.VMEM((3, width, width), BF16),
            pltpu.VMEM((3, mid, width), BF16),
            pltpu.VMEM((3, 16, mid), BF16),
            pltpu.VMEM((3, tall, width), BF16),
            dma((3, 6)),
            dma((6,)),
            dma((4,)),
            dma((2, 3)),
            dma((2, 3)),
            dma((2, 3)),
            dma((2, 3, len(parts))),
        ],
        compiler_params=pltpu.CompilerParams(
            collective_id=0, has_side_effects=True, vmem_limit_bytes=48 * 2**20
        ),
        name="exchange",
    )(*(pltpu.with_memory_space_constraint(a, pltpu.HBM) for a in (
        constraint[0, 0, 0],
        stiff_ib[0, 0, 0],
        mass_ib[0, 0, 0],
        mass_ii.reshape(1, depth),
        modes[0, 0, 0],
        stiff_faces[0, 0, 0],
        mass_faces[0, 0, 0],
        dof_map[0, 0, 0][:, None],
    )))
    outs = pl.pallas_call(
        write_out,
        out_shape=[jax.ShapeDtypeStruct(shape, BF16) for shape in shapes],
        in_specs=[vmem] * 3,
        out_specs=[hbm] * 3,
        scratch_shapes=[dma((3, 3))],
        compiler_params=pltpu.CompilerParams(vmem_limit_bytes=2**20),
        name="write_out",
    )(*(pltpu.with_memory_space_constraint(b, pltpu.VMEM) for b in blocks))
    return tuple(out[None, None, None] for out in outs)


def solution(mesh):
    sizes = tuple(mesh.shape[name] for name in AXES)
    grid = P("gx", "gy", "gz")
    return jax.shard_map(
        functools.partial(local, sizes),
        mesh=mesh,
        in_specs=(grid,) * 8,
        out_specs=(grid,) * 3,
        check_vma=False,
    )
```

time: 93.3 us -> 47.4 us (0.51)
  the two profiles are of different devices: /device:TPU:111 before, /device:TPU:175 now
where the time goes in v1:
time: 47.4 us; the launch traced here: 47.3 us
  Pallas kernels  46.7 us (99%)
  between operations  0.64 us (1%)
    pallas_call x1, Pallas kernels, local(): pl.pallas_call(functools.partial(exchange, sizes, parts), out_shape=[pltp...  44.3 us
    pallas_call x1, Pallas kernels, local(): pl.pallas_call(write_out, out_shape=[jax.ShapeDtypeStruct(shape, BF16) fo...  2.34 us

profile of v1, /device:TPU:175, one launch (start us, length us, event | category | flops | bytes accessed | tf_op | source)
XLA Modules:
  0.0 47.3 jit_solution(10906134255879221968)
XLA Ops:
  0.6 44.3 %exchange.1 = (bf16[3,512,512]{2,1,0:T(8,128)(2,1)S(1)}, bf16[3,512,512]{2,1,0:T(8,128)(2,1)S(1)}, bf16[3,600,512]{2,1,0:T(8,128)(2,1)S(1)}) custom-call(bf16[256,3072]{1,0:T(8,128)(2,1)} %bitcast.12, bf16[256,3072]{1,0:T(8,128)(2,1)} %bitcast.13, bf16[256,3072]{1,0:T(8,128)(2,1)} %bitcast.14, f32[1,256]{1,0:T(1,128)} %bitcast.18, ...), custom_call_target="tpu_custom_call" | custom-call | tf_op jit(solution)/shard_map/exchange/pallas_call | solution.py:337
  45.0 2.3 %write_out.1 = (bf16[3,512,512]{2,1,0:T(8,128)(2,1)}, bf16[3,512,512]{2,1,0:T(8,128)(2,1)}, bf16[3,600,512]{2,1,0:T(8,128)(2,1)}) custom-call(bf16[3,512,512]{2,1,0:T(8,128)(2,1)S(1)} %get-tuple-element.9.stiff_in, bf16[3,512,512]{2,1,0:T(8,128)(2,1)S(1)} %get-tuple-element.10.mass_in, bf16[3,600,512]{2,1,0:T(8,128)(2,1)S(1)} %get-tuple-element.11.coup_in), custom_call_target="tpu_custom_call" | custom-call | tf_op jit(solution)/shard_map/write_out/pallas_call | solution.py:388
